TPU v7x, 32 devices: a whole 2x2x4 slice. The times are simulated.
32 devices in a mesh: sub: 2 (over y), row: 4 (over x, core), col: 4 (over z).
Axes of the slice: x: 2, y: 2, z: 4, core: 2. Of those that a mesh axis runs over, the one named last changes fastest.
Arguments:
- visibility: bfloat16 [2, 16, 512, 4096], P(None, 'sub', 'row', 'col'), may hold values from -13 to 13
- sky_model: bfloat16 [2, 16, 512, 4096], P(None, 'sub', 'row', 'col'), may hold values from -4 to 4, as said below
- antenna_flags: int32 [2, 512], P('sub'), may hold values 0 or 1
- gains_init: float32 [2, 16, 512], P(None, 'sub'), may hold values from -0.5 to 1.5
Outputs:
- gains: float32 [2, 16, 512], P(None, 'sub')
Inputs may be any that keep to these rules, and one draw needn't show every extreme that they name: `sky_model`: model visibility parts lie between -4 and 4.
All inputs are finite; a program needn't handle non-finite values.
Results may differ from a plain program's by a relative error of at most 0.0003.
Values sent between devices are 32-bit elements.
A program may use at most 64 MiB of HBM per device.

v0:
```python
import jax
import jax.numpy as jnp
from jax import lax
from jax.sharding import PartitionSpec as P

TIMES = 8
ITERS = 3


def subband_total(values):
    return lax.psum(values, "sub")


def update_gains(summed, previous):
    denominator = summed[:, 2, :] + 1.0
    quotient = jnp.stack([summed[:, 0, :] / denominator, summed[:, 1, :] / denominator], axis=0)
    updated = 0.5 * (quotient + previous)
    chan_mean = jnp.sum(updated, axis=1) / updated.shape[1]
    overall = subband_total(chan_mean) / lax.axis_size("sub")
    return updated + 0.5 * (overall - chan_mean)[:, None, :]


def time_total(values, selector):
    return jnp.einsum(
        "crk,kq->crq",
        values,
        selector,
        precision=lax.Precision.HIGHEST,
        preferred_element_type=jnp.float32,
    )


def contract(matrix, vector):
    return jnp.einsum("cpq,cq->cp", matrix, vector, precision=lax.Precision.HIGHEST)


def body(visibility, sky_model, antenna_flags, gains_init):
    block_rows = visibility.shape[2]
    wide_cols = visibility.shape[3]
    block_cols = wide_cols // TIMES
    row_at = lax.axis_index("row") * block_rows
    col_at = lax.axis_index("col") * block_cols
    flag_value = antenna_flags[0].astype(jnp.float32)
    row_flag = lax.dynamic_slice_in_dim(flag_value, row_at, block_rows)
    col_flag = lax.dynamic_slice_in_dim(flag_value, col_at, block_cols)
    row_ids = row_at + lax.iota(jnp.int32, block_rows)
    col_ids = col_at + lax.iota(jnp.int32, block_cols)
    weight = (
        row_flag[:, None]
        * col_flag[None, :]
        * (row_ids[:, None] != col_ids[None, :]).astype(jnp.float32)
    )
    selector = (
        lax.iota(jnp.int32, wide_cols)[:, None] // TIMES == lax.iota(jnp.int32, block_cols)[None, :]
    ).astype(jnp.float32)
    vis_re = visibility[0].astype(jnp.float32)
    vis_im = visibility[1].astype(jnp.float32)
    mod_re = sky_model[0].astype(jnp.float32)
    mod_im = sky_model[1].astype(jnp.float32)
    cross_re = time_total(vis_re * mod_re + vis_im * mod_im, selector) * weight
    cross_im = time_total(vis_im * mod_re - vis_re * mod_im, selector) * weight
    power_sum = time_total(mod_re * mod_re + mod_im * mod_im, selector) * weight
    gain_values = gains_init
    for step_index in range(ITERS):
        col_gains = lax.dynamic_slice_in_dim(gain_values, col_at, block_cols, 2)
        gain_re = col_gains[0]
        gain_im = col_gains[1]
        num_re = contract(cross_re, gain_re) - contract(cross_im, gain_im)
        num_im = contract(cross_re, gain_im) + contract(cross_im, gain_re)
        denominator = contract(power_sum, gain_re * gain_re + gain_im * gain_im)
        partial_value = jnp.stack([num_re, num_im, denominator], axis=1)
        summed = lax.psum(partial_value, "col")
        previous = lax.dynamic_slice_in_dim(gain_values, row_at, block_rows, 2)
        gain_block = update_gains(summed, previous)
        gain_values = lax.all_gather(gain_block, "row", axis=2, tiled=True)
    return gain_values


def solution(mesh):
    return jax.shard_map(
        body,
        mesh=mesh,
        in_specs=(
            P(None, "sub", "row", "col"),
            P(None, "sub", "row", "col"),
            P("sub", None),
            P(None, "sub", None),
        ),
        out_specs=P(None, "sub", None),
        check_vma=False,
    )
```

profile of v0, /device:TPU:0, one launch (start us, length us, event | category | flops | bytes accessed | tf_op | source)
XLA Modules:
  0.0 111.2 jit_solution(4182115625880762958)
XLA Ops:
  1.5 6.6 %fusion.25 = f32[8,128,128]{2,1,0:T(8,128)S(1)} fusion(bf16[2,8,128,1024]{3,2,1,0:T(8,128)(2,1)} %param.4, bf16[2,8,128,1024]{3,2,1,0:T(8,128)(2,1)} %param.5, f32[128,128]{1,0:T(8,128)S(1)} %multiply_select_fusion, s32[1024]{0:T(1024)S(1)} %add_select_fusion), kind=kOutput, calls=%fused_computation.26 | convolution fusion | flops 1618214912 | bytes 8982528 | tf_op jit(solution)/shard_map/crk,kq->crq/dot_general | solution.py:24
  8.1 0.9 fusion.61
  9.0 0.9 fusion.59
  10.0 3.0 %fusion.28 = f32[8,128,128]{2,1,0:T(8,128)S(1)} fusion(bf16[2,8,128,1024]{3,2,1,0:T(8,128)(2,1)S(1)} %copy-done.1, bf16[2,8,128,1024]{3,2,1,0:T(8,128)(2,1)S(1)} %copy-done.2, f32[128,128]{1,0:T(8,128)S(1)} %multiply_select_fusion, s32[1024]{0:T(1024)S(1)} %add_select_fusion), kind=kOutput, calls=%fused_computation.27 | convolution fusion | flops 1618214912 | bytes 8982528 | tf_op jit(solution)/shard_map/crk,kq->crq/dot_general | solution.py:24
  13.9 0.9 fusion.58
  14.8 2.7 %fusion.22 = f32[8,128,128]{2,1,0:T(8,128)S(1)} fusion(bf16[2,8,128,1024]{3,2,1,0:T(8,128)(2,1)S(1)} %copy-done.2, f32[128,128]{1,0:T(8,128)S(1)} %multiply_select_fusion, s32[1024]{0:T(1024)S(1)} %add_select_fusion), kind=kOutput, calls=%fused_computation.25 | convolution fusion | flops 1616117760 | bytes 4788224 | tf_op jit(solution)/shard_map/crk,kq->crq/dot_general | solution.py:24
  17.5 0.9 fusion.62
  18.4 20.4 %psum.42 = f32[8,3,128]{2,0,1:T(8,128)S(1)} all-reduce(f32[8,3,128]{2,0,1:T(8,128)S(1)} %pad_maximum_fusion), channel_id=1, replica_groups=mesh['sub'=2,'row'=4,'col'=4] {'col'}, use_global_device_ids=true, to_apply=%region_0.1 | all-reduce | flops 3072 | bytes 24576 | tf_op jit(solution)/shard_map/psum | solution.py:72
  38.9 4.9 %psum.43 = f32[2,128]{1,0:T(2,128)S(1)} all-reduce(f32[2,128]{1,0:T(2,128)S(1)} %broadcast_multiply_fusion.2), channel_id=1, replica_groups=mesh['sub'=2,'row'=4,'col'=4] {'sub'}, use_global_device_ids=true, to_apply=%region_2.3 | all-reduce | flops 256 | bytes 2048 | tf_op jit(solution)/shard_map/psum | solution.py:11
  43.9 5.2 %all_gather.9 = f32[2,8,512]{2,1,0:T(8,128)S(1)} all-gather(f32[2,8,128]{2,1,0:T(8,128)S(1)} %broadcast_add_fusion.2), channel_id=1, replica_groups=mesh['sub'=2,'row'=4,'col'=4] {'row'}, dimensions={2}, use_global_device_ids=true | all-gather | bytes 40960 | tf_op jit(solution)/shard_map/all_gather | solution.py:75
  50.0 0.9 fusion.66
  50.9 0.9 fusion.63
  51.8 0.9 fusion.65
  52.8 0.9 fusion.64
  53.7 15.5 %psum.44 = f32[8,3,128]{2,0,1:T(8,128)S(1)} all-reduce(f32[8,3,128]{2,0,1:T(8,128)S(1)} %pad_maximum_fusion.1), channel_id=1, replica_groups=mesh['sub'=2,'row'=4,'col'=4] {'col'}, use_global_device_ids=true, to_apply=%region_3.4 | all-reduce | flops 3072 | bytes 24576 | tf_op jit(solution)/shard_map/psum | solution.py:72
  69.3 4.9 %psum.45 = f32[2,128]{1,0:T(2,128)S(1)} all-reduce(f32[2,128]{1,0:T(2,128)S(1)} %broadcast_multiply_fusion.1), channel_id=1, replica_groups=mesh['sub'=2,'row'=4,'col'=4] {'sub'}, use_global_device_ids=true, to_apply=%region_5.6 | all-reduce | flops 256 | bytes 2048 | tf_op jit(solution)/shard_map/psum | solution.py:11
  74.3 5.2 %all_gather.10 = f32[2,8,512]{2,1,0:T(8,128)S(1)} all-gather(f32[2,8,128]{2,1,0:T(8,128)S(1)} %broadcast_add_fusion.1), channel_id=1, replica_groups=mesh['sub'=2,'row'=4,'col'=4] {'row'}, dimensions={2}, use_global_device_ids=true | all-gather | bytes 40960 | tf_op jit(solution)/shard_map/all_gather | solution.py:75
  80.4 0.9 fusion.71
  81.3 0.9 fusion.69
  82.2 0.9 fusion.70
  83.2 0.9 fusion.68
  84.1 16.2 %psum.46 = f32[8,3,128]{2,0,1:T(8,128)S(1)} all-reduce(f32[8,3,128]{2,0,1:T(8,128)S(1)} %pad_maximum_fusion.2), channel_id=1, replica_groups=mesh['sub'=2,'row'=4,'col'=4] {'col'}, use_global_device_ids=true, to_apply=%region_6.7 | all-reduce | flops 3072 | bytes 24576 | tf_op jit(solution)/shard_map/psum | solution.py:72
  100.4 4.9 %psum.47 = f32[2,128]{1,0:T(2,128)S(1)} all-reduce(f32[2,128]{1,0:T(2,128)S(1)} %broadcast_multiply_fusion), channel_id=1, replica_groups=mesh['sub'=2,'row'=4,'col'=4] {'sub'}, use_global_device_ids=true, to_apply=%region_8.9 | all-reduce | flops 256 | bytes 2048 | tf_op jit(solution)/shard_map/psum | solution.py:11
  105.3 5.2 %all_gather.11 = f32[2,8,512]{2,1,0:T(8,128)S(1)} all-gather(f32[2,8,128]{2,1,0:T(8,128)S(1)} %broadcast_add_fusion), channel_id=1, replica_groups=mesh['sub'=2,'row'=4,'col'=4] {'row'}, dimensions={2}, use_global_device_ids=true | all-gather | bytes 40960 | tf_op jit(solution)/shard_map/all_gather | solution.py:75
  (42 shorter events, 5.1 us)
Async XLA Ops:
  1.5 8.4 %copy-start.1 = (bf16[2,8,128,1024]{3,2,1,0:T(8,128)(2,1)S(1)}, bf16[2,8,128,1024]{3,2,1,0:T(8,128)(2,1)}, u32[]{:S(2)}) copy-start(bf16[2,8,128,1024]{3,2,1,0:T(8,128)(2,1)} %param.4) | copy-start | bytes 12582916
  1.5 8.4 %copy-start.2 = (bf16[2,8,128,1024]{3,2,1,0:T(8,128)(2,1)S(1)}, bf16[2,8,128,1024]{3,2,1,0:T(8,128)(2,1)}, u32[]{:S(2)}) copy-start(bf16[2,8,128,1024]{3,2,1,0:T(8,128)(2,1)} %param.5) | copy-start | bytes 12582916
  13.9 25.0 %copy-start = (f32[2,8,512]{2,1,0:T(8,128)S(1)}, f32[2,8,512]{2,1,0:T(8,128)}, u32[]{:S(2)}) copy-start(f32[2,8,512]{2,1,0:T(8,128)} %param.7) | copy-start | bytes 98308
where the time goes:
time: 112 us; the launch traced here: 111 us
  blocking collectives  82.5 us (74%)
  matrix products  26.1 us (23%)
  other arithmetic  1.73 us (2%)
    psum x3, blocking collectives, body(): summed = lax.psum(partial_value, 'col')  52.2 us
    all_gather x3, blocking collectives, body(): gain_values = lax.all_gather(gain_block, 'row', axis=2, tiled=True)  15.6 us
    psum x3, blocking collectives, subband_total(): return lax.psum(values, 'sub')  14.8 us
    dot_general x15, matrix products, contract(): jnp.einsum('cpq,cq->cp', matrix, vector, precision=lax.Precision.HIGHEST)  13.9 us
    dot_general x3, matrix products, time_total(): jnp.einsum('crk,kq->crq', values, selector, precision=lax.Precision.HIGHE...  12.3 us

commit v1 on v0

v1 whole, which is shorter than its diff:
```python
import functools

import jax
import jax.numpy as jnp
from jax import lax
from jax.experimental import pallas as pl
from jax.experimental.pallas import tpu as pltpu
from jax.sharding import PartitionSpec as P

TIMES = 8
ITERS = 3
MESH = pl.DeviceIdType.MESH


def pick_block(value, index, count, width):
    picked = value[..., :width]
    for block in range(1, count):
        picked = jnp.where(index == block, value[..., block * width : (block + 1) * width], picked)
    return picked


def kernel(
    n_sub,
    n_row,
    n_col,
    vis_hbm,
    sky_hbm,
    flags_hbm,
    gains_hbm,
    out_ref,
    vis,
    sky,
    flags,
    gains,
    mats,
    own_gains,
    part_buf,
    prev_buf,
    upd_buf,
    mean_buf,
    last_upd,
    last_mean,
    load_sem,
    part_send,
    part_recv,
    prev_send,
    prev_recv,
    upd_send,
    upd_recv,
    mean_send,
    mean_recv,
    last_upd_send,
    last_upd_recv,
    last_mean_send,
    last_mean_recv,
):
    sub = lax.axis_index("sub")
    row = lax.axis_index("row")
    col = lax.axis_index("col")
    chans, block_rows, wide = vis.shape[1:]
    block_cols = wide // TIMES

    def load_vis(c):
        return pltpu.make_async_copy(vis_hbm.at[:, c], vis.at[:, c], load_sem.at[0, c])

    def load_sky(c):
        return pltpu.make_async_copy(sky_hbm.at[:, c], sky.at[:, c], load_sem.at[1, c])

    load_flags = pltpu.make_async_copy(flags_hbm, flags, load_sem.at[0, chans])
    load_gains = pltpu.make_async_copy(gains_hbm, gains, load_sem.at[1, chans])
    for c in range(chans):
        load_vis(c).start()
        load_sky(c).start()
    load_flags.start()
    load_gains.start()

    barrier = pltpu.get_barrier_semaphore()
    for step in range(1, n_col):
        pl.semaphore_signal(
            barrier, inc=1, device_id=(sub, row, lax.rem(col + step, n_col)), device_id_type=MESH
        )
    for sub_step in range(n_sub):
        for row_step in range(n_row):
            if sub_step or row_step:
                other = (lax.rem(sub + sub_step, n_sub), lax.rem(row + row_step, n_row), col)
                pl.semaphore_signal(barrier, inc=1, device_id=other, device_id_type=MESH)

    tile = min(256, wide)
    tile_cols = tile // TIMES
    selector = (
        lax.broadcasted_iota(jnp.int32, (tile_cols, tile), 1) // TIMES
        == lax.broadcasted_iota(jnp.int32, (tile_cols, tile), 0)
    ).astype(jnp.bfloat16)
    row_ids = row * block_rows + lax.broadcasted_iota(jnp.int32, (tile_cols, block_rows), 1)
    col_ids = col * block_cols + lax.broadcasted_iota(jnp.int32, (tile_cols, block_rows), 0)

    def time_total(values):
        high = values.astype(jnp.bfloat16)
        low = (values - high.astype(jnp.float32)).astype(jnp.bfloat16)
        dims = (((1,), (1,)), ((), ()))
        return lax.dot_general(
            selector, high, dims, preferred_element_type=jnp.float32
        ) + lax.dot_general(selector, low, dims, preferred_element_type=jnp.float32)

    def prepare(c, carry):
        load_vis(c).wait()
        load_sky(c).wait()
        for j in range(wide // tile):
            at = slice(j * tile, (j + 1) * tile)
            vis_re = vis[0, c, :, at].astype(jnp.float32)
            vis_im = vis[1, c, :, at].astype(jnp.float32)
            mod_re = sky[0, c, :, at].astype(jnp.float32)
            mod_im = sky[1, c, :, at].astype(jnp.float32)
            off_diagonal = row_ids != col_ids + j * tile_cols
            to = slice(j * tile_cols, (j + 1) * tile_cols)
            cross_re = time_total(vis_re * mod_re + vis_im * mod_im)
            mats[0, c, to, :] = jnp.where(off_diagonal, cross_re, 0.0)
            cross_im = time_total(vis_im * mod_re - vis_re * mod_im)
            mats[1, c, to, :] = jnp.where(off_diagonal, cross_im, 0.0)
            power = time_total(mod_re * mod_re + mod_im * mod_im)
            mats[2, c, to, :] = jnp.where(off_diagonal, power, 0.0)
        return carry

    lax.fori_loop(0, chans, prepare, 0)

    load_flags.wait()
    load_gains.wait()
    flag_value = flags[...].astype(jnp.float32)
    row_flag = pick_block(flag_value, row, n_row, block_rows)
    col_flag = pick_block(flag_value, col, n_col, block_cols)

    def partial_sums(step, gain_re, gain_im):
        gain_re = (gain_re * col_flag).T
        gain_im = (gain_im * col_flag).T
        for c in range(chans):
            one_re = gain_re[:, c : c + 1]
            one_im = gain_im[:, c : c + 1]
            cross_re, cross_im, power = mats[0, c], mats[1, c], mats[2, c]
            at = (step, col)
            part_buf[(*at, 0, pl.ds(c, 1))] = jnp.sum(
                cross_re * one_re - cross_im * one_im, axis=0, keepdims=True
            )
            part_buf[(*at, 1, pl.ds(c, 1))] = jnp.sum(
                cross_re * one_im + cross_im * one_re, axis=0, keepdims=True
            )
            part_buf[(*at, 2, pl.ds(c, 1))] = jnp.sum(
                power * (one_re * one_re + one_im * one_im), axis=0, keepdims=True
            )

    def send_part(step, source, target, index):
        return pltpu.make_async_remote_copy(
            src_ref=part_buf.at[step, source],
            dst_ref=part_buf.at[step, source],
            send_sem=part_send.at[step, index],
            recv_sem=part_recv.at[step, source],
            device_id=(sub, row, target),
            device_id_type=MESH,
        )

    def send_prev(target, index):
        return pltpu.make_async_remote_copy(
            src_ref=prev_buf,
            dst_ref=prev_buf,
            send_sem=prev_send.at[index],
            recv_sem=prev_recv,
            device_id=(sub, row, target),
            device_id_type=MESH,
        )

    def send_upd(step, target, index):
        return pltpu.make_async_remote_copy(
            src_ref=upd_buf.at[step],
            dst_ref=upd_buf.at[step],
            send_sem=upd_send.at[step, index],
            recv_sem=upd_recv.at[step],
            device_id=(sub, target, col),
            device_id_type=MESH,
        )

    def send_mean(step, source, target, index):
        return pltpu.make_async_remote_copy(
            src_ref=mean_buf.at[step, source],
            dst_ref=mean_buf.at[step, source],
            send_sem=mean_send.at[(step, *index)],
            recv_sem=mean_recv.at[step, source],
            device_id=(*target, col),
            device_id_type=MESH,
        )

    def send_last_upd(source, target, index):
        return pltpu.make_async_remote_copy(
            src_ref=last_upd.at[source],
            dst_ref=last_upd.at[source],
            send_sem=last_upd_send.at[index],
            recv_sem=last_upd_recv.at[source],
            device_id=(sub, target, col),
            device_id_type=MESH,
        )

    def send_last_mean(source, target, index):
        return pltpu.make_async_remote_copy(
            src_ref=last_mean.at[source[0], source[1]],
            dst_ref=last_mean.at[source[0], source[1]],
            send_sem=last_mean_send.at[index[0], index[1]],
            recv_sem=last_mean_recv.at[source[0], source[1]],
            device_id=(*target, col),
            device_id_type=MESH,
        )

    def others(me, count):
        return [(step, lax.rem(me + step, count)) for step in range(1, count)]

    def everyone(me, count):
        return [(step, lax.rem(me + step, count)) for step in range(count)]

    def update(step, previous):
        total = part_buf[step, 0]
        for source in range(1, n_col):
            total = total + part_buf[step, source]
        denominator = total[2] * row_flag + 1.0
        upd_re = 0.5 * (total[0] * row_flag / denominator + previous[0])
        upd_im = 0.5 * (total[1] * row_flag / denominator + previous[1])
        return upd_re, upd_im

    def chan_mean(value):
        return jnp.sum(value, axis=0, keepdims=True) / chans

    home = row == col
    gain_re = pick_block(gains[0], col, n_col, block_cols)
    gain_im = pick_block(gains[1], col, n_col, block_cols)

    for step in range(ITERS):
        last = step == ITERS - 1
        if last:
            @pl.when(home)
            def _():
                prev_buf[0] = gain_re
                prev_buf[1] = gain_im
                for index, target in others(col, n_col):
                    send_prev(target, index).start()

        partial_sums(step, gain_re, gain_im)
        if step == 0:
            pl.semaphore_wait(barrier, n_col - 1 + n_sub * n_row - 1)

        if not last:
            own_gains[0] = gain_re
            own_gains[1] = gain_im

            @pl.when(jnp.logical_not(home))
            def _():
                send_part(step, col, row, 0).start()
                send_upd(step, row, 0).wait_recv()

            @pl.when(home)
            def _():
                for index, source in others(col, n_col):
                    send_part(step, source, col, 0).wait_recv()
                upd_re, upd_im = update(step, own_gains)
                mean_buf[step, sub, 0] = chan_mean(upd_re)
                mean_buf[step, sub, 1] = chan_mean(upd_im)
                upd_buf[step, 0] = upd_re
                upd_buf[step, 1] = upd_im
                for sub_index, sub_target in others(sub, n_sub):
                    for row_index, row_target in everyone(row, n_row):
                        send_mean(step, sub, (sub_target, row_target), (sub_index, row_index)).start()
                for index, target in others(row, n_row):
                    send_upd(step, target, index).start()

            upd_re = upd_buf[step, 0]
            upd_im = upd_buf[step, 1]
            mean_re = chan_mean(upd_re)
            mean_im = chan_mean(upd_im)

            @pl.when(jnp.logical_not(home))
            def _():
                mean_buf[step, sub, 0] = mean_re
                mean_buf[step, sub, 1] = mean_im

            for index, source in others(sub, n_sub):
                send_mean(step, source, (sub, row), (0, 0)).wait_recv()
            overall = mean_buf[step, 0]
            for source in range(1, n_sub):
                overall = overall + mean_buf[step, source]
            overall = overall / n_sub
            gain_re = upd_re + 0.5 * (overall[0] - mean_re)
            gain_im = upd_im + 0.5 * (overall[1] - mean_im)
        else:
            for index, target in others(col, n_col):
                send_part(step, col, target, index).start()

            @pl.when(jnp.logical_not(home))
            def _():
                send_prev(col, 0).wait_recv()

            for index, source in others(col, n_col):
                send_part(step, source, col, 0).wait_recv()
            upd_re, upd_im = update(step, prev_buf)
            last_mean[sub, row, 0] = chan_mean(upd_re)
            last_mean[sub, row, 1] = chan_mean(upd_im)
            last_upd[row, 0] = upd_re
            last_upd[row, 1] = upd_im
            for sub_index, sub_target in others(sub, n_sub):
                for row_index, row_target in everyone(row, n_row):
                    send_last_mean(
                        (sub, row), (sub_target, row_target), (sub_index, row_index)
                    ).start()
            for index, target in others(row, n_row):
                send_last_upd(row, target, index).start()
            for index, source in others(row, n_row):
                send_last_upd(source, row, 0).wait_recv()
                last_mean[sub, source, 0] = chan_mean(last_upd[source, 0])
                last_mean[sub, source, 1] = chan_mean(last_upd[source, 1])
            for sub_index, sub_source in others(sub, n_sub):
                for row_index, row_source in everyone(row, n_row):
                    send_last_mean((sub_source, row_source), (sub, row), (0, 0)).wait_recv()
            for block in range(n_row):
                overall = last_mean[0, block]
                for source in range(1, n_sub):
                    overall = overall + last_mean[source, block]
                overall = overall / n_sub
                shift = 0.5 * (overall - last_mean[sub, block])
                at = slice(block * block_rows, (block + 1) * block_rows)
                out_ref[0, :, at] = last_upd[block, 0] + shift[0]
                out_ref[1, :, at] = last_upd[block, 1] + shift[1]

    for step in range(ITERS - 1):
        @pl.when(jnp.logical_not(home))
        def _():
            send_part(step, col, row, 0).wait_send()

        @pl.when(home)
        def _():
            for sub_index, sub_target in others(sub, n_sub):
                for row_index, row_target in everyone(row, n_row):
                    send_mean(
                        step, sub, (sub_target, row_target), (sub_index, row_index)
                    ).wait_send()
            for index, target in others(row, n_row):
                send_upd(step, target, index).wait_send()

    @pl.when(home)
    def _():
        for index, target in others(col, n_col):
            send_prev(target, index).wait_send()

    for index, target in others(col, n_col):
        send_part(ITERS - 1, col, target, index).wait_send()
    for sub_index, sub_target in others(sub, n_sub):
        for row_index, row_target in everyone(row, n_row):
            send_last_mean(
                (sub, row), (sub_target, row_target), (sub_index, row_index)
            ).wait_send()
    for index, target in others(row, n_row):
        send_last_upd(row, target, index).wait_send()


def body(n_sub, n_row, n_col, visibility, sky_model, antenna_flags, gains_init):
    chans, block_rows, wide = visibility.shape[1:]
    block_cols = wide // TIMES
    assert n_row == n_col and block_rows == block_cols
    dma = pltpu.SemaphoreType.DMA
    part = (chans, block_rows)
    mean = (2, 1, block_rows)
    return pl.pallas_call(
        functools.partial(kernel, n_sub, n_row, n_col),
        out_shape=jax.ShapeDtypeStruct(gains_init.shape, jnp.float32),
        in_specs=[pl.BlockSpec(memory_space=pl.ANY)] * 4,
        out_specs=pl.BlockSpec(memory_space=pltpu.VMEM),
        scratch_shapes=[
            pltpu.VMEM(visibility.shape, visibility.dtype),
            pltpu.VMEM(sky_model.shape, sky_model.dtype),
            pltpu.VMEM(antenna_flags.shape, antenna_flags.dtype),
            pltpu.VMEM(gains_init.shape, jnp.float32),
            pltpu.VMEM((3, chans, block_cols, block_rows), jnp.float32),
            pltpu.VMEM((2, *part), jnp.float32),
            pltpu.VMEM((ITERS, n_col, 3, *part), jnp.float32),
            pltpu.VMEM((2, *part), jnp.float32),
            pltpu.VMEM((ITERS - 1, 2, *part), jnp.float32),
            pltpu.VMEM((ITERS - 1, n_sub, *mean), jnp.float32),
            pltpu.VMEM((n_row, 2, *part), jnp.float32),
            pltpu.VMEM((n_sub, n_row, *mean), jnp.float32),
            dma((2, chans + 1)),
            dma((ITERS, n_col)),
            dma((ITERS, n_col)),
            dma((n_col,)),
            dma(()),
            dma((ITERS - 1, n_row)),
            dma((ITERS - 1,)),
            dma((ITERS - 1, n_sub, n_row)),
            dma((ITERS - 1, n_sub)),
            dma((n_row,)),
            dma((n_row,)),
            dma((n_sub, n_row)),
            dma((n_sub, n_row)),
        ],
        compiler_params=pltpu.CompilerParams(
            collective_id=0, has_side_effects=True, vmem_limit_bytes=67_000_000
        ),
    )(visibility, sky_model, antenna_flags, gains_init)


def solution(mesh):
    return jax.shard_map(
        functools.partial(body, mesh.shape["sub"], mesh.shape["row"], mesh.shape["col"]),
        mesh=mesh,
        in_specs=(
            P(None, "sub", "row", "col"),
            P(None, "sub", "row", "col"),
            P("sub", None),
            P(None, "sub", None),
        ),
        out_specs=P(None, "sub", None),
        check_vma=False,
    )
```

time: 112 us -> 34.1 us (0.30)
  blocking collectives: 82.5 us -> 0 us
  Pallas kernels: 0 us -> 32.5 us
  matrix products: 26.1 us -> 0 us
  other arithmetic: 1.73 us -> 0 us
    psum x6 -> x0, blocking collectives: 67 us -> none  [the longest x3 52.2 us: body(): summed = lax.psum(partial_value, 'col')]
    pallas_call x0 -> x1, Pallas kernels: none -> 32.5 us  [body(): pl.pallas_call(functools.partial(kernel, n_sub, n_row, n_col), out_shape=...]
    dot_general x18 -> x0, matrix products: 26.1 us -> none  [the longest x15 13.9 us: contract(): jnp.einsum('cpq,cq->cp', matrix, vector, precision=lax.Precision.HIGHEST)]
    all_gather x3 -> x0, blocking collectives: 15.6 us -> none  [body(): gain_values = lax.all_gather(gain_block, 'row', axis=2, tiled=True)]
where the time goes in v1:
time: 34.1 us; the launch traced here: 33.9 us
  Pallas kernels  32.5 us (95%)
  local copies, waits for them, and re-layouts  1.38 us (4%)
    pallas_call x1, Pallas kernels, body(): pl.pallas_call(functools.partial(kernel, n_sub, n_row, n_col), out_shape=...  32.5 us
    unnamed x1, local copies, waits for them, and re-layouts  1.38 us

profile of v1, /device:TPU:0, one launch (start us, length us, event | category | flops | bytes accessed | tf_op | source)
XLA Modules:
  0.0 33.9 jit_solution(4069263088976501837)
XLA Ops:
  0.0 32.5 %shard_map.46 = f32[2,8,512]{2,1,0:T(8,128)} custom-call(bf16[2,8,128,1024]{3,2,1,0:T(8,128)(2,1)} %vis_hbm.1, bf16[2,8,128,1024]{3,2,1,0:T(8,128)(2,1)} %sky_hbm.1, s32[1,512]{1,0:T(1,128)} %flags_hbm.1, f32[2,8,512]{2,1,0:T(8,128)} %gains_hbm.1), custom_call_target="tpu_custom_call" | custom-call | tf_op jit(solution)/shard_map/pallas_call | solution.py:365
  32.6 1.4 %copy.6 = f32[2,8,512]{2,1,0:T(8,128)} copy(f32[2,8,512]{2,1,0:T(8,128)} %shard_map.46) | data formatting | bytes 65536
